TPU v7x, 32 devices: a whole 2x2x4 slice. The times are simulated.
32 devices in a mesh: rep: 4 (over z), row: 2 (over x), col: 4 (over y, core).
Axes of the slice: x: 2, y: 2, z: 4, core: 2. Of those that a mesh axis runs over, the one named last changes fastest.
Arguments:
- grad_parts: bfloat16 [4, 8192, 8192], P('rep', 'row', 'col'), may hold values from -6 to 6
- momentum: float32 [8192, 8192], P(('row', 'rep'), 'col'), may hold values from -24 to 24
- basis: float32 [8192, 384], P('col'), may hold values from -0.0625 to 0.0625
Outputs:
- update: bfloat16 [8192, 8192], P('row', 'col')
- new_momentum: float32 [8192, 8192], P(('row', 'rep'), 'col')
- new_basis: float32 [8192, 384], P('col')
- power_norms: float32 [384], replicated
All inputs are finite; a program needn't handle non-finite values.
Results may differ from a plain program's by a relative error of at most 0.0085.
Values may be sent and summed in bfloat16 or wider, within the bound.
No kernel may reach another device: no remote copies, remote signals or barrier semaphores. Data moves between devices by JAX's collectives and lax.ppermute only.
A program may use at most 128 MiB of HBM per device.

v0:
```python
import jax
import jax.numpy as jnp
from jax import lax
from jax.sharding import PartitionSpec as P

D = 8192
RANK = 384
EPS = 1e-06
FEEDBACK = 0.05
HIGH = lax.Precision.HIGHEST


def local(grad_parts, momentum, basis):
    replicas = lax.axis_size("rep")
    local_grad = grad_parts[0].astype(jnp.float32)
    summed = lax.psum_scatter(
        local_grad.astype(jnp.bfloat16), "rep", scatter_dimension=0, tiled=True
    ).astype(jnp.float32)
    blended = momentum + summed / replicas
    power = jnp.dot(blended, basis, precision=HIGH)
    power = lax.psum(power, "col")
    squares = lax.psum(jnp.sum(power * power, axis=0), ("rep", "row"))
    power_norms = jnp.sqrt(squares / D)
    scaled = power / (jnp.sqrt(squares) + EPS)
    gram = lax.psum(jnp.dot(scaled.T, scaled, precision=HIGH), ("rep", "row"))
    factor = jnp.linalg.cholesky(gram)
    orth = jax.scipy.linalg.solve_triangular(factor, scaled.T, lower=True).T
    tile_orth = lax.all_gather(orth, "rep", axis=0, tiled=True)
    back = jnp.dot(blended.T, orth, precision=HIGH)
    back = lax.psum(back, ("rep", "row"))
    back_squares = lax.psum(jnp.sum(back * back, axis=0), "col")
    new_basis = back / (jnp.sqrt(back_squares) + EPS)
    new_momentum = blended - FEEDBACK * jnp.dot(orth, back.T, precision=HIGH)
    scale = D / RANK**0.5
    update = (scale * jnp.dot(tile_orth, new_basis.T, precision=HIGH)).astype(jnp.bfloat16)
    return (update, new_momentum, new_basis, power_norms)


def solution(mesh):
    placed = (P("rep", "row", "col"), P(("row", "rep"), "col"), P("col", None))
    return jax.shard_map(
        local,
        mesh=mesh,
        in_specs=placed,
        out_specs=(P("row", "col"), P(("row", "rep"), "col"), P("col", None), P()),
        check_vma=False,
    )
```

profile of v0, /device:TPU:0, one launch (start us, length us, event | category | flops | bytes accessed | tf_op | source)
XLA Modules:
  0.0 922.6 jit_solution(1023822813130225376)
XLA Ops:
  8.0 285.6 %reduce-scatter.2.cloned.1.call-done = bf16[1024,2048]{1,0:T(8,128)(2,1)} async-done(((bf16[4096,2048]{1,0:T(8,128)(2,1)}), bf16[1024,2048]{1,0:T(8,128)(2,1)}) %reduce-scatter.2.cloned.1.call-update) | async-done | bytes 4194320 | tf_op jit(solution)/shard_map/reduce_scatter | solution.py:16
  293.5 17.7 %fusion.1 = f32[1024,384]{1,0:T(8,128)} fusion(f32[2048,384]{1,0:T(8,128)S(1)} %copy-done, f32[1024,2048]{1,0:T(8,128)} %param.4, bf16[1024,2048]{1,0:T(8,128)(2,1)} %reduce-scatter.2.cloned.1.call-done), kind=kOutput, calls=%fused_computation.7 | convolution fusion | flops 9669967872 | bytes 17301504 | tf_op jit(solution)/shard_map/dot_general | solution.py:20
  311.3 43.6 %all-reduce.5.cloned.1.call-done = f32[1024,384]{1,0:T(8,128)} async-done(((f32[1024,384]{1,0:T(8,128)}), f32[1024,384]{1,0:T(8,128)}) %all-reduce.5.cloned.1.call-update) | async-done | bytes 1572880 | tf_op jit(solution)/shard_map/psum | solution.py:21
  354.9 1.6 multiply_reduce_fusion.1
  356.5 21.4 %psum.36 = f32[384]{0:T(512)S(1)} all-reduce(f32[384]{0:T(512)S(1)} %multiply_reduce_fusion.1), channel_id=1, replica_groups=mesh['rep'=4,'row'=2,'col'=4] {'rep','row'}, use_global_device_ids=true, to_apply=%region_3.0 | all-reduce | flops 384 | bytes 3072 | tf_op jit(solution)/shard_map/psum | solution.py:22
  378.5 5.6 fusion.7
  384.4 69.4 %all-reduce.7.cloned.1.call-done = f32[384,384]{0,1:T(8,128)} async-done(((f32[384,384]{0,1:T(8,128)}), f32[384,384]{0,1:T(8,128)}) %all-reduce.7.cloned.1.call-update) | async-done | bytes 589840 | tf_op jit(solution)/shard_map/psum | solution.py:25
  453.9 1.3 copy.8
  455.1 1.1 fusion.8
  456.3 11.7 %cholesky.77 = f32[128,128]{1,0:T(8,128)S(1)} custom-call(f32[128,128]{1,0:T(8,128)S(1)} %cholesky.192), custom_call_target="Cholesky" | custom-call | tf_op jit(solution)/shard_map/jit(cholesky)/cholesky | solution.py:26
  468.0 9.8 %custom-call.23 = f32[1,128,128]{1,2,0:T(8,128)S(1)} custom-call(f32[1,128,128]{2,1,0:T(8,128)S(1)} %get-tuple-element.28), custom_call_target="InvertDiagBlocksLowerTriangular" | custom-call | tf_op jit(solution)/shard_map/jit(cholesky)/cholesky | solution.py:26
  478.5 11.7 %cholesky.162 = f32[128,128]{1,0:T(8,128)S(1)} custom-call(f32[128,128]{1,0:T(8,128)S(1)} %cholesky.196), custom_call_target="Cholesky" | custom-call | tf_op jit(solution)/shard_map/jit(cholesky)/cholesky | solution.py:26
  490.2 10.2 %custom-call.24 = f32[1,128,128]{1,2,0:T(8,128)S(1)} custom-call(f32[1,128,128]{2,1,0:T(8,128)S(1)} %get-tuple-element.25), custom_call_target="InvertDiagBlocksLowerTriangular" | custom-call | tf_op jit(solution)/shard_map/jit(cholesky)/cholesky | solution.py:26
  500.9 11.7 %cholesky.181 = f32[128,128]{1,0:T(8,128)S(1)} custom-call(f32[128,128]{1,0:T(8,128)S(1)} %convolution_subtract_fusion.3), custom_call_target="Cholesky" | custom-call | tf_op jit(solution)/shard_map/jit(cholesky)/cholesky | solution.py:26
  512.7 0.7 compare_reduce_fusion
  516.1 6.0 while.1
  516.7 1.4 bitcast_dynamic-update-slice_fusion.2
  518.7 1.4 bitcast_dynamic-update-slice_fusion.2
  520.7 1.4 bitcast_dynamic-update-slice_fusion.2
  522.1 29.5 %custom-call.25 = f32[3,128,128]{1,2,0:T(8,128)S(1)} custom-call(f32[3,128,128]{2,1,0:T(8,128)S(1)} %get-tuple-element.11), custom_call_target="InvertDiagBlocksLowerTriangular" | custom-call | tf_op jit(solution)/shard_map/jit(_solve_triangular)/triangular_solve | solution.py:27
  552.3 1.0 convolution_subtract_fusion.1
  553.9 2.9 convolution_subtract_fusion
  557.5 30.4 %fusion = f32[2048,384]{1,0:T(8,128)} fusion(f32[1024,2048]{1,0:T(8,128)} %param.4, bf16[1024,2048]{1,0:T(8,128)(2,1)S(1)} %copy-done.2, f32[128,1024]{1,0:T(8,128)S(1)} %fusion.15, f32[128,1024]{1,0:T(8,128)S(1)} %fusion.17, f32[128,1024]{1,0:T(8,128)S(1)} %fusion.9), kind=kOutput, calls=%fused_computation.6 | convolution fusion | flops 9670754304 | bytes 17301504 | tf_op jit(solution)/shard_map/dot_general | solution.py:29
  588.0 1.3 fusion.5
  589.3 126.5 %all-reduce.9.cloned.1.call-done = f32[2048,384]{1,0:T(8,128)} async-done(((f32[2048,384]{1,0:T(8,128)}), f32[2048,384]{1,0:T(8,128)}) %all-reduce.9.cloned.1.call-update) | async-done | bytes 3145744 | tf_op jit(solution)/shard_map/psum | solution.py:30
  715.8 2.3 multiply_reduce_fusion
  718.1 6.2 psum.39
  724.4 1.9 broadcast_divide_fusion
  726.3 1.7 copy-done.3
  728.6 23.8 %multiply_subtract_fusion = f32[1024,2048]{1,0:T(8,128)} fusion(f32[2048,384]{1,0:T(8,128)S(1)} %copy-done.4, f32[1024,2048]{1,0:T(8,128)} %param.4, bf16[1024,2048]{1,0:T(8,128)(2,1)S(1)} %copy-done.3, f32[128,1024]{1,0:T(8,128)S(1)} %copy-done.10, f32[128,1024]{1,0:T(8,128)S(1)} %copy-done.8, f32[128,1024]{1,0:T(8,128)S(1)} %copy-done.6), kind=kOutput, calls=%fused_computation.3 | convolution fusion | flops 9674948608 | bytes 25690112 | tf_op jit(solution)/shard_map/dot_general | solution.py:33
  752.3 79.8 %all-gather.2.cloned.1.call-done = f32[4096,384]{0,1:T(8,128)} async-done(((f32[1024,384]{0,1:T(8,128)}), f32[4096,384]{0,1:T(8,128)}) %all-gather.2.cloned.1.call-update) | async-done | bytes 6291472 | tf_op jit(solution)/shard_map/all_gather | solution.py:28
  832.2 83.8 %multiply_convert_fusion = bf16[4096,2048]{1,0:T(8,128)(2,1)} fusion(f32[4096,384]{0,1:T(8,128)} %all-gather.2.cloned.1.call-done, f32[2048,384]{1,0:T(8,128)} %broadcast_divide_fusion), kind=kOutput, calls=%fused_computation.2 | convolution fusion | flops 38671482880 | bytes 26214400 | tf_op jit(solution)/shard_map/dot_general | solution.py:35
  (62 shorter events, 8.0 us)
Async XLA Ops:
  7.2 286.4 %copy-start = (f32[2048,384]{1,0:T(8,128)S(1)}, f32[2048,384]{1,0:T(8,128)}, u32[]{:S(2)}) copy-start(f32[2048,384]{1,0:T(8,128)} %param.5) | copy-start | bytes 9437188
  7.2 286.4 %reduce-scatter.2.cloned.1.call-start = ((), (), s32[]{:S(2)}) async-start(), calls=%async_computation.1 | async-start | bytes 20971520 | tf_op jit(solution)/shard_map/reduce_scatter | solution.py:16
  7.9 347.0 %all-reduce.5.cloned.1.call-start = ((), (), s32[]{:S(2)}) async-start(), calls=%async_computation.2 | async-start | bytes 3145728 | tf_op jit(solution)/shard_map/psum | solution.py:21
  311.3 142.6 %all-reduce.7.cloned.1.call-start = ((), (), s32[]{:S(2)}) async-start(), calls=%async_computation.3 | async-start | bytes 1179648 | tf_op jit(solution)/shard_map/psum | solution.py:25
  378.5 5.8 copy-start.11
  384.0 331.7 %all-reduce.9.cloned.1.call-start = ((), (), s32[]{:S(2)}) async-start(), calls=%async_computation.5 | async-start | bytes 6291456 | tf_op jit(solution)/shard_map/psum | solution.py:30
  522.1 30.2 %copy-start.12 = (f32[384,384]{1,0:T(8,128)}, f32[384,384]{1,0:T(8,128)S(1)}, u32[]{:S(2)}) copy-start(f32[384,384]{1,0:T(8,128)S(1)} %get-tuple-element.96) | copy-start | bytes 1769476
  552.3 35.7 %copy-start.5 = (f32[128,1024]{1,0:T(8,128)}, f32[128,1024]{1,0:T(8,128)S(1)}, u32[]{:S(2)}) copy-start(f32[128,1024]{1,0:T(8,128)S(1)} %fusion.9) | copy-start | bytes 1572868
  552.3 5.2 copy-start.2
  553.9 34.0 %copy-start.7 = (f32[128,1024]{1,0:T(8,128)}, f32[128,1024]{1,0:T(8,128)S(1)}, u32[]{:S(2)}) copy-start(f32[128,1024]{1,0:T(8,128)S(1)} %fusion.17) | copy-start | bytes 1572868
  557.5 30.5 %copy-start.9 = (f32[128,1024]{1,0:T(8,128)}, f32[128,1024]{1,0:T(8,128)S(1)}, u32[]{:S(2)}) copy-start(f32[128,1024]{1,0:T(8,128)S(1)} %fusion.15) | copy-start | bytes 1572868
  587.9 244.3 %all-gather.2.cloned.1.call-start = ((), (), s32[]{:S(2)}) async-start(), calls=%async_computation.4 | async-start | bytes 7864320 | tf_op jit(solution)/shard_map/all_gather | solution.py:28
  715.8 8.6 copy-start.4
  724.3 3.6 copy-start.3
  724.4 3.8 copy-start.6
  724.4 4.0 copy-start.8
  724.4 4.2 copy-start.10
  832.2 83.8 %copy-start.1 = (f32[2048,384]{1,0:T(8,128)S(1)}, f32[2048,384]{1,0:T(8,128)}, u32[]{:S(2)}) copy-start(f32[2048,384]{1,0:T(8,128)} %param.5) | copy-start | bytes 9437188
Sparse Core Ops, SparseCore 0:
  10.3 283.1 reduce-scatter.1
  311.4 43.4 all-reduce.4
  384.2 69.6 all-reduce.6
  588.0 127.7 all-reduce.8
  717.8 114.3 all-gather.1
where the time goes:
time: 930 us; the launch traced here: 923 us
  waiting for transfers between devices  606 us (65%)
  matrix products  168 us (18%)
  other arithmetic  95.1 us (10%)
  blocking collectives  27.6 us (3%)
  between operations  16.3 us (2%)
  local copies, waits for them, and re-layouts  9.64 us (1%)
    reduce_scatter x1, waiting for transfers between devices, local(): lax.psum_scatter(local_grad.astype(jnp.bfloat16), 'rep', scatter_dimensio...  286 us
    psum x1, waiting for transfers between devices, local(): back = lax.psum(back, ('rep', 'row'))  126 us
    dot_general x1, matrix products, local(): jnp.dot(tile_orth, new_basis.T, precision=HIGH)  83.8 us
    all_gather x1, waiting for transfers between devices, local(): tile_orth = lax.all_gather(orth, 'rep', axis=0, tiled=True)  79.8 us
    psum x1, waiting for transfers between devices, local(): gram = lax.psum(jnp.dot(scaled.T, scaled, precision=HIGH), ('rep', 'row'))  69.4 us
    another operation x10, other arithmetic, local(): factor = jnp.linalg.cholesky(gram)  56.6 us
    psum x1, waiting for transfers between devices, local(): power = lax.psum(power, 'col')  43.6 us
    dot_general x1, matrix products, local(): back = jnp.dot(blended.T, orth, precision=HIGH)  30.4 us
  transfers between devices with their start and end apart: 5, of which 5 were waited for; matrix products, arithmetic and copies ran while one was open for 3% of the time, Pallas kernels for 0%

commit v1 on v0

--- a/solution.py
+++ b/solution.py
@@ -1,3 +1,4 @@
+import functools
 import jax
 import jax.numpy as jnp
 from jax import lax
@@ -8,6 +9,22 @@
 EPS = 1e-06
 FEEDBACK = 0.05
 HIGH = lax.Precision.HIGHEST
+
+
+def plane_handle(local_x, axis_id):
+    fields = [local_x]
+    world = lax.psum(1, axis_id)
+    for kk in range(world - 1):
+        fields.append(
+            lax.ppermute(fields[-1], axis_id, [(it, (it + 1) % world) for it in range(world)])
+        )
+    block_out = jnp.roll(
+        jnp.concatenate(fields[::-1], 0), (lax.axis_index(axis_id) + 1) * local_x.shape[0], axis=0
+    )
+    return block_out
+
+
+loads_attach = functools.partial(plane_handle, axis_id="rep")
 
 
 def local(grad_parts, momentum, basis):
@@ -25,7 +42,7 @@
     gram = lax.psum(jnp.dot(scaled.T, scaled, precision=HIGH), ("rep", "row"))
     factor = jnp.linalg.cholesky(gram)
     orth = jax.scipy.linalg.solve_triangular(factor, scaled.T, lower=True).T
-    tile_orth = lax.all_gather(orth, "rep", axis=0, tiled=True)
+    tile_orth = loads_attach(orth)
     back = jnp.dot(blended.T, orth, precision=HIGH)
     back = lax.psum(back, ("rep", "row"))
     back_squares = lax.psum(jnp.sum(back * back, axis=0), "col")

time: 930 us -> 909 us (0.977)
  waiting for transfers between devices: 606 us -> 584 us
    all_gather x1 -> x0, waiting for transfers between devices: 79.8 us -> none  [local(): tile_orth = lax.all_gather(orth, 'rep', axis=0, tiled=True)]
    ppermute x0 -> x3, waiting for transfers between devices: none -> 75.9 us  [plane_handle(): lax.ppermute(fields[-1], axis_id, [(it, (it + 1) % world) for it in range...]
    psum x1, waiting for transfers between devices: 126 us -> 108 us  [local(): back = lax.psum(back, ('rep', 'row'))]
  transfers between devices with their start and end apart: 5 -> 7, of which waited for: 5 -> 6; matrix products, arithmetic and copies ran while one was open for 3% -> 3% of each run, Pallas kernels for 0% -> 0%
where the time goes in v1:
time: 909 us; the launch traced here: 902 us
  waiting for transfers between devices  584 us (64%)
  matrix products  167 us (18%)
  other arithmetic  94.3 us (10%)
  blocking collectives  27.6 us (3%)
  between operations  16.2 us (2%)
  local copies, waits for them, and re-layouts  11.8 us (1%)
    reduce_scatter x1, waiting for transfers between devices, local(): lax.psum_scatter(local_grad.astype(jnp.bfloat16), 'rep', scatter_dimensio...  286 us
    psum x1, waiting for transfers between devices, local(): back = lax.psum(back, ('rep', 'row'))  108 us
    dot_general x1, matrix products, local(): jnp.dot(tile_orth, new_basis.T, precision=HIGH)  81.5 us
    ppermute x3, waiting for transfers between devices, plane_handle(): lax.ppermute(fields[-1], axis_id, [(it, (it + 1) % world) for it in range...  75.9 us
    psum x1, waiting for transfers between devices, local(): gram = lax.psum(jnp.dot(scaled.T, scaled, precision=HIGH), ('rep', 'row'))  69.4 us
    another operation x10, other arithmetic, local(): factor = jnp.linalg.cholesky(gram)  56.5 us
    psum x1, waiting for transfers between devices, local(): power = lax.psum(power, 'col')  43.6 us
    dot_general x1, matrix products, local(): back = jnp.dot(blended.T, orth, precision=HIGH)  30.4 us
  transfers between devices with their start and end apart: 7, of which 6 were waited for; matrix products, arithmetic and copies ran while one was open for 3% of the time, Pallas kernels for 0%

profile of v1, /device:TPU:0, one launch (start us, length us, event | category | flops | bytes accessed | tf_op | source)
XLA Modules:
  0.0 901.9 jit_solution(3877934317788511689)
XLA Ops:
  8.0 285.6 %reduce-scatter.2.cloned.1.call-done = bf16[1024,2048]{1,0:T(8,128)(2,1)} async-done(((bf16[4096,2048]{1,0:T(8,128)(2,1)}), bf16[1024,2048]{1,0:T(8,128)(2,1)}) %reduce-scatter.2.cloned.1.call-update) | async-done | bytes 4194320 | tf_op jit(solution)/shard_map/reduce_scatter | solution.py:33
  293.5 17.7 %fusion.2 = f32[1024,384]{1,0:T(8,128)} fusion(f32[2048,384]{1,0:T(8,128)S(1)} %copy-done, f32[1024,2048]{1,0:T(8,128)} %param.4, bf16[1024,2048]{1,0:T(8,128)(2,1)} %reduce-scatter.2.cloned.1.call-done), kind=kOutput, calls=%fused_computation.8 | convolution fusion | flops 9669967872 | bytes 17301504 | tf_op jit(solution)/shard_map/dot_general | solution.py:37
  311.3 43.6 %all-reduce.5.cloned.1.call-done = f32[1024,384]{1,0:T(8,128)} async-done(((f32[1024,384]{1,0:T(8,128)}), f32[1024,384]{1,0:T(8,128)}) %all-reduce.5.cloned.1.call-update) | async-done | bytes 1572880 | tf_op jit(solution)/shard_map/psum | solution.py:38
  354.9 1.6 multiply_reduce_fusion.1
  356.5 21.4 %psum.36 = f32[384]{0:T(512)S(1)} all-reduce(f32[384]{0:T(512)S(1)} %multiply_reduce_fusion.1), channel_id=1, replica_groups=mesh['rep'=4,'row'=2,'col'=4] {'rep','row'}, use_global_device_ids=true, to_apply=%region_3.0 | all-reduce | flops 384 | bytes 3072 | tf_op jit(solution)/shard_map/psum | solution.py:39
  378.5 5.6 fusion.8
  384.5 69.4 %all-reduce.7.cloned.1.call-done = f32[384,384]{0,1:T(8,128)} async-done(((f32[384,384]{0,1:T(8,128)}), f32[384,384]{0,1:T(8,128)}) %all-reduce.7.cloned.1.call-update) | async-done | bytes 589840 | tf_op jit(solution)/shard_map/psum | solution.py:42
  453.9 1.3 copy.8
  455.2 1.1 fusion.9
  456.3 11.7 %cholesky.77 = f32[128,128]{1,0:T(8,128)S(1)} custom-call(f32[128,128]{1,0:T(8,128)S(1)} %cholesky.192), custom_call_target="Cholesky" | custom-call | tf_op jit(solution)/shard_map/jit(cholesky)/cholesky | solution.py:43
  468.1 9.8 %custom-call.23 = f32[1,128,128]{1,2,0:T(8,128)S(1)} custom-call(f32[1,128,128]{2,1,0:T(8,128)S(1)} %get-tuple-element.28), custom_call_target="InvertDiagBlocksLowerTriangular" | custom-call | tf_op jit(solution)/shard_map/jit(cholesky)/cholesky | solution.py:43
  478.5 11.7 %cholesky.162 = f32[128,128]{1,0:T(8,128)S(1)} custom-call(f32[128,128]{1,0:T(8,128)S(1)} %cholesky.196), custom_call_target="Cholesky" | custom-call | tf_op jit(solution)/shard_map/jit(cholesky)/cholesky | solution.py:43
  490.3 10.2 %custom-call.24 = f32[1,128,128]{1,2,0:T(8,128)S(1)} custom-call(f32[1,128,128]{2,1,0:T(8,128)S(1)} %get-tuple-element.25), custom_call_target="InvertDiagBlocksLowerTriangular" | custom-call | tf_op jit(solution)/shard_map/jit(cholesky)/cholesky | solution.py:43
  500.9 11.7 %cholesky.181 = f32[128,128]{1,0:T(8,128)S(1)} custom-call(f32[128,128]{1,0:T(8,128)S(1)} %convolution_subtract_fusion.3), custom_call_target="Cholesky" | custom-call | tf_op jit(solution)/shard_map/jit(cholesky)/cholesky | solution.py:43
  516.0 6.0 while.1
  516.6 1.4 bitcast_dynamic-update-slice_fusion.2
  518.6 1.4 bitcast_dynamic-update-slice_fusion.2
  520.6 1.4 bitcast_dynamic-update-slice_fusion.2
  522.0 29.5 %custom-call.25 = f32[3,128,128]{1,2,0:T(8,128)S(1)} custom-call(f32[3,128,128]{2,1,0:T(8,128)S(1)} %get-tuple-element.11), custom_call_target="InvertDiagBlocksLowerTriangular" | custom-call | tf_op jit(solution)/shard_map/jit(_solve_triangular)/triangular_solve | solution.py:44
  552.2 1.0 convolution_subtract_fusion.1
  553.8 2.7 convolution_subtract_fusion
  557.2 30.4 %fusion.1 = f32[2048,384]{1,0:T(8,128)} fusion(f32[1024,2048]{1,0:T(8,128)} %param.4, bf16[1024,2048]{1,0:T(8,128)(2,1)S(1)} %copy-done.2, f32[128,1024]{1,0:T(8,128)S(1)} %fusion.16, f32[128,1024]{1,0:T(8,128)S(1)} %fusion.18, f32[128,1024]{1,0:T(8,128)S(1)} %fusion.10), kind=kOutput, calls=%fused_computation.7 | convolution fusion | flops 9670754304 | bytes 17301504 | tf_op jit(solution)/shard_map/dot_general | solution.py:46
  588.3 66.8 %collective-permute-done = f32[1024,384]{0,1:T(8,128)S(1)} collective-permute-done((f32[1024,384]{0,1:T(8,128)S(1)}, f32[1024,384]{0,1:T(8,128)S(1)}, u32[]{:S(2)}, u32[]{:S(2)}) %collective-permute-start) | collective-permute-done | bytes 1572896 | tf_op jit(solution)/shard_map/ppermute | solution.py:19
  655.3 108.5 %all-reduce.9.cloned.1.call-done = f32[2048,384]{1,0:T(8,128)} async-done(((f32[2048,384]{1,0:T(8,128)}), f32[2048,384]{1,0:T(8,128)}) %all-reduce.9.cloned.1.call-update) | async-done | bytes 3145744 | tf_op jit(solution)/shard_map/psum | solution.py:47
  763.8 2.2 multiply_reduce_fusion
  766.0 6.2 psum.39
  772.5 2.3 broadcast_divide_fusion
  775.6 25.1 %multiply_subtract_fusion = f32[1024,2048]{1,0:T(8,128)} fusion(f32[2048,384]{1,0:T(8,128)} %all-reduce.9.cloned.1.call-done, f32[1024,2048]{1,0:T(8,128)} %param.4, bf16[1024,2048]{1,0:T(8,128)(2,1)S(1)} %copy-done.3, f32[128,1024]{1,0:T(8,128)S(1)} %fusion.16, f32[128,1024]{1,0:T(8,128)S(1)} %fusion.18, f32[128,1024]{1,0:T(8,128)S(1)} %fusion.10), kind=kOutput, calls=%fused_computation.3 | convolution fusion | flops 9674948608 | bytes 25690112 | tf_op jit(solution)/shard_map/dot_general | solution.py:50
  800.8 9.1 %collective-permute-done.2 = f32[1024,384]{0,1:T(8,128)S(1)} collective-permute-done((f32[1024,384]{0,1:T(8,128)}, f32[1024,384]{0,1:T(8,128)S(1)}, u32[]{:S(2)}, u32[]{:S(2)}) %collective-permute-start.2) | collective-permute-done | bytes 1572896 | tf_op jit(solution)/shard_map/ppermute | solution.py:19
  810.0 1.5 constant_dynamic-update-slice_fusion.6
  811.9 1.5 constant_dynamic-update-slice_fusion.2
  813.7 81.5 %multiply_convert_fusion = bf16[4096,2048]{1,0:T(8,128)(2,1)} fusion(f32[2048,384]{1,0:T(8,128)S(1)} %broadcast_divide_fusion, f32[8192,384]{0,1:T(8,128)S(1)} %constant_dynamic-update-slice_fusion, s32[]{:T(128)S(6)} %select_n.19), kind=kOutput, calls=%fused_computation.2 | convolution fusion | flops 38671482880 | bytes 26214404 | tf_op jit(solution)/shard_map/dot_general | solution.py:52
  (61 shorter events, 10.8 us)
Async XLA Ops:
  7.2 286.4 %copy-start = (f32[2048,384]{1,0:T(8,128)S(1)}, f32[2048,384]{1,0:T(8,128)}, u32[]{:S(2)}) copy-start(f32[2048,384]{1,0:T(8,128)} %param.5) | copy-start | bytes 9437188
  7.2 286.4 %reduce-scatter.2.cloned.1.call-start = ((), (), s32[]{:S(2)}) async-start(), calls=%async_computation.1 | async-start | bytes 20971520 | tf_op jit(solution)/shard_map/reduce_scatter | solution.py:33
  7.9 347.0 %all-reduce.5.cloned.1.call-start = ((), (), s32[]{:S(2)}) async-start(), calls=%async_computation.2 | async-start | bytes 3145728 | tf_op jit(solution)/shard_map/psum | solution.py:38
  311.3 142.6 %all-reduce.7.cloned.1.call-start = ((), (), s32[]{:S(2)}) async-start(), calls=%async_computation.3 | async-start | bytes 1179648 | tf_op jit(solution)/shard_map/psum | solution.py:42
  378.5 5.9 copy-start.4
  384.1 379.7 %all-reduce.9.cloned.1.call-start = ((), (), s32[]{:S(2)}) async-start(), calls=%async_computation.4 | async-start | bytes 6291456 | tf_op jit(solution)/shard_map/psum | solution.py:47
  522.0 30.2 %copy-start.6 = (f32[384,384]{1,0:T(8,128)}, f32[384,384]{1,0:T(8,128)S(1)}, u32[]{:S(2)}) copy-start(f32[384,384]{1,0:T(8,128)S(1)} %get-tuple-element.96) | copy-start | bytes 1769476
  552.1 5.0 copy-start.2
  587.7 67.4 %collective-permute-start = (f32[1024,384]{0,1:T(8,128)S(1)}, f32[1024,384]{0,1:T(8,128)S(1)}, u32[]{:S(2)}, u32[]{:S(2)}) collective-permute-start(f32[1024,384]{0,1:T(8,128)S(1)} %fusion.6), channel_id=1, source_target_pairs={{0,8},{8,16},{16,24},{24,0},{1,9},{9,17},{17,25},{25,1},{2,10},{10... | collective-permute-start | bytes 4718600 | tf_op jit(solution)/shard_map/ppermute | solution.py:19
  655.1 117.0 %collective-permute-start.1 = (f32[1024,384]{0,1:T(8,128)S(1)}, f32[1024,384]{0,1:T(8,128)}, u32[]{:S(2)}, u32[]{:S(2)}) collective-permute-start(f32[1024,384]{0,1:T(8,128)S(1)} %collective-permute-done), channel_id=1, source_target_pairs={{0,8},{8,16},{16,24},{24,0},{1,9},{9,17},{17,25},{25,1},{2,10},{10... | collective-permute-start | bytes 4718600 | tf_op jit(solution)/shard_map/ppermute | solution.py:19
  772.2 37.6 %collective-permute-start.2 = (f32[1024,384]{0,1:T(8,128)}, f32[1024,384]{0,1:T(8,128)S(1)}, u32[]{:S(2)}, u32[]{:S(2)}) collective-permute-start(f32[1024,384]{0,1:T(8,128)} %collective-permute-done.1), channel_id=1, source_target_pairs={{0,8},{8,16},{16,24},{24,0},{1,9},{9,17},{17,25},{25,1},{2,10},{10... | collective-permute-start | bytes 4718600 | tf_op jit(solution)/shard_map/ppermute | solution.py:19
  772.5 3.1 copy-start.3
  775.6 38.1 %copy-start.5 = (f32[2048,384]{1,0:T(8,128)}, f32[2048,384]{1,0:T(8,128)S(1)}, u32[]{:S(2)}) copy-start(f32[2048,384]{1,0:T(8,128)S(1)} %broadcast_divide_fusion) | copy-start | bytes 9437188
  813.7 81.5 %copy-start.1 = (f32[2048,384]{1,0:T(8,128)S(1)}, f32[2048,384]{1,0:T(8,128)}, u32[]{:S(2)}) copy-start(f32[2048,384]{1,0:T(8,128)} %param.5) | copy-start | bytes 9437188
Sparse Core Ops, SparseCore 0:
  10.3 283.1 reduce-scatter.1
  311.4 43.4 all-reduce.4
  384.2 69.6 all-reduce.6
  587.7 176.0 all-reduce.8
